TPU v7x, 256 devices: a whole 4x4x8 slice. The times are simulated.
256 devices in a mesh: row: 32 (over y, z), col: 8 (over x, core).
Axes of the slice: x: 4, y: 4, z: 8, core: 2. Of those that a mesh axis runs over, the one named last changes fastest.
Arguments:
- grams: bfloat16 [4, 3584, 3584], P(None, 'row', 'col'), as said below
- weights: bfloat16 [4, 3584, 7168], P(None, 'row', 'col'), may hold values from -6 to 6
Outputs:
- merged: float32 [3584, 7168], P('row', 'col')
- residual: float32 [3584, 7168], P('row', 'col')
Inputs may be any that keep to these rules, and one draw needn't show every extreme that they name: `grams`: each of the 4 matrices is symmetric and positive definite.
All inputs are finite; a program needn't handle non-finite values.
Results may differ from a plain program's by a relative error of at most 0.012.
The roundings to bfloat16 on the way count: a program that leaves them out, or rounds other values in their place, can miss the bound.
Values may be sent and summed in bfloat16 or wider, within the bound.
A program may use at most 256 MiB of HBM per device.

v0:
```python
import jax
import jax.numpy as jnp
from jax import lax
from jax.sharding import Mesh
from jax.sharding import PartitionSpec as P

ITERS = 2
ROW = ("row_0", "row_1")


def sum_by_axis(so_far, axes):
    for axis in axes:
        so_far = lax.psum_scatter(so_far, axis, scatter_dimension=0, tiled=True)
    return so_far


def sent_to_all(x, axis):
    copies = jnp.broadcast_to(x, (lax.axis_size(axis), *x.shape))
    return lax.all_to_all(copies, axis, split_axis=0, concat_axis=0, tiled=True)


def of_everyone(x, axis):
    return sent_to_all(x, axis).sum(axis=0)


def together(arrays, axis):
    ravelled, at, done = (jnp.concatenate([a.reshape(-1) for a in arrays]), 0, [])
    so_far = of_everyone(ravelled, axis)
    for a in arrays:
        done.append(so_far[at : at + a.size].reshape(a.shape))
        at += a.size
    return tuple(done)


def shards(grams, weights):
    slab_rows = grams.shape[1]
    col_count = weights.shape[2]
    first_row = lax.axis_index(ROW) * slab_rows
    high = lax.Precision.HIGHEST
    gram_slabs = lax.all_gather(grams, "col", axis=2, tiled=True)
    gram_total = jnp.sum(gram_slabs, axis=0, dtype=jnp.float32)
    square_block = lax.dynamic_slice_in_dim(gram_slabs, first_row, slab_rows, gram_slabs.ndim - 1)
    diag_total = jnp.einsum(
        "mr,mrc->rc",
        jnp.diagonal(square_block, axis1=-2, axis2=-1).astype(jnp.float32),
        weights.astype(jnp.float32),
    )
    product = sum_by_axis(
        jnp.einsum("mrk,mrc->kc", gram_slabs, weights, preferred_element_type=jnp.float32), ROW
    )
    right_side = 0.9 * product + 0.1 * diag_total
    total_diag = jnp.diagonal(lax.dynamic_slice_in_dim(gram_total, first_row, slab_rows, 1))
    merged = jnp.zeros((slab_rows, col_count), jnp.float32)
    residual = right_side
    direction = right_side
    for iteration in range(ITERS):
        rounded = direction.astype(jnp.bfloat16)
        shard_piece = lax.all_gather(rounded, ROW, axis=0, tiled=True)
        add_columns = lax.slice_in_dim(gram_total, 0, shard_piece.shape[0], axis=1)
        mapped = jnp.zeros((slab_rows, col_count), jnp.float32) + jnp.dot(
            add_columns, shard_piece.astype(jnp.float32), precision=high
        )
        mapped = 0.9 * mapped + 0.1 * total_diag[:, None] * rounded.astype(jnp.float32)
        curvature, cross_term, square, norm_now = together(
            (
                jnp.sum(direction * mapped, axis=0),
                jnp.sum(residual * mapped, axis=0),
                jnp.sum(mapped * mapped, axis=0),
                jnp.sum(residual * residual, axis=0),
            ),
            ROW,
        )
        step_length = norm_now / curvature
        merged = merged + step_length * direction
        residual = residual - step_length * mapped
        if iteration + 1 < ITERS:
            norm_next = (
                norm_now - 2.0 * step_length * cross_term + step_length * step_length * square
            )
            direction = residual + norm_next / norm_now * direction
    return (merged, residual)


def solution(mesh):
    torus = Mesh(mesh.devices.reshape(4, 8, mesh.shape["col"]), ("row_0", "row_1", "col"))
    in_specs = (P(None, ROW, "col"), P(None, ROW, "col"))
    out_specs = (P(ROW, "col"), P(ROW, "col"))
    return jax.shard_map(
        shards, mesh=torus, in_specs=in_specs, out_specs=out_specs, check_vma=False
    )
```

profile of v0, /device:TPU:32, one launch (start us, length us, event | category | flops | bytes accessed | tf_op | source)
XLA Modules:
  0.0 467.3 jit_solution(11836406161750740182)
XLA Ops:
  7.2 0.0 copy-start
  7.2 0.0 all-gather.4.cloned.1.call-start
  7.2 2.1 copy.14
  9.3 0.0 all-gather.4.cloned.1.call-update
  9.3 0.0 reduce-scatter.3.cloned.1.call-start
  9.4 35.5 %all-gather.4.cloned.1.call-done = bf16[4,112,3584]{1,2,0:T(8,128)(2,1)} async-done(((bf16[4,112,448]{1,2,0:T(8,128)(2,1)}), bf16[4,112,3584]{1,2,0:T(8,128)(2,1)}) %all-gather.4.cloned.1.call-update) | async-done | bytes 3211280 | tf_op jit(solution)/shard_map/all_gather | solution.py:40
  44.9 0.0 copy-done
  44.9 8.9 %convolution_bitcast_fusion = f32[3584,896]{1,0:T(8,128)} fusion(bf16[4,112,3584]{1,2,0:T(8,128)(2,1)} %all-gather.4.cloned.1.call-done, bf16[4,112,896]{2,1,0:T(8,128)(2,1)S(1)} %copy-done), kind=kOutput, calls=%fused_computation.2 | convolution fusion | flops 2877292544 | bytes 16859136 | tf_op jit(solution)/shard_map/mrk,mrc->kc/dot_general | solution.py:49
  53.7 0.0 reduce-scatter.3.cloned.1.call-update
  53.8 0.0 reduce-scatter.5.cloned.1.call-start
  53.8 119.3 %reduce-scatter.3.cloned.1.call-done = f32[896,896]{1,0:T(8,128)} async-done(((f32[3584,896]{1,0:T(8,128)}), f32[896,896]{1,0:T(8,128)}) %reduce-scatter.3.cloned.1.call-update) | async-done | bytes 3211280 | tf_op jit(solution)/shard_map/reduce_scatter | solution.py:13
  173.1 0.0 reduce-scatter.5.cloned.1.call-update
  173.1 0.0 all-gather.6.cloned.1.call-start
  173.2 0.9 constant_dynamic-slice_fusion.1
  174.1 3.2 copy.15
  177.3 2.9 gather_fusion
  180.2 0.6 fusion.2
  180.8 41.3 %reduce-scatter.5.cloned.1.call-done = f32[112,896]{1,0:T(8,128)} async-done(((f32[896,896]{1,0:T(8,128)}), f32[112,896]{1,0:T(8,128)}) %reduce-scatter.5.cloned.1.call-update) | async-done | bytes 401424 | tf_op jit(solution)/shard_map/reduce_scatter | solution.py:13
  222.1 1.8 fusion.10
  223.9 0.0 copy-start.1
  223.9 0.0 all-gather.6.cloned.1.call-update
  223.9 0.0 all-gather.8.cloned.1.call-start
  223.9 3.0 convert_reduce_fusion
  227.0 0.1 copy.24
  227.1 1.7 gather_fusion.1
  228.8 85.2 %all-gather.6.cloned.1.call-done = bf16[3584,896]{1,0:T(8,128)(2,1)} async-done(((bf16[112,896]{1,0:T(8,128)(2,1)}), bf16[3584,896]{1,0:T(8,128)(2,1)}) %all-gather.6.cloned.1.call-update) | async-done | bytes 6422544 | tf_op jit(solution)/shard_map/all_gather | solution.py:58
  314.0 0.0 copy-done.1
  314.0 7.0 %multiply_reduce_fusion.6 = (f32[896]{0:T(1024)S(1)}, f32[896]{0:T(1024)S(1)}, f32[896]{0:T(1024)S(1)}, f32[112,896]{1,0:T(8,128)}) fusion(f32[112,896]{1,0:T(8,128)S(1)} %get-tuple-element.14, bf16[112,896]{1,0:T(8,128)(2,1)S(1)} %copy-done.1, f32[112]{0:T(128)S(1)} %broadcast_multiply_fusion, f32[112,3584]{0,1:T(8,128)S(1)} %convert_reduce_fusion, ...), kind=kOutput, calls=%fused_computation.22 | convolution fusion | flops 4316939776 | bytes 9042880 | tf_op jit(solution)/shard_map/dot_general | solution.py:60
  320.9 0.2 broadcast_in_dim.12
  321.2 21.5 %all_to_all.12 = f32[32,1,3584]{2,1,0:T(1,128)S(1)} all-to-all(f32[32,1,3584]{2,1,0:T(1,128)S(1)} %broadcast_in_dim.12), channel_id=1, replica_groups=mesh['row_0'=4,'row_1'=8,'col'=8] {'row_0','row_1'}, dimensions={0} | all-to-all | bytes 917504 | tf_op jit(solution)/shard_map/all_to_all | solution.py:19
  342.7 0.3 reduce_sum.98
  343.0 1.7 fusion.5
  344.8 0.0 all-gather.8.cloned.1.call-update
  344.8 84.9 %all-gather.8.cloned.1.call-done = bf16[3584,896]{1,0:T(8,128)(2,1)} async-done(((bf16[112,896]{1,0:T(8,128)(2,1)}), bf16[3584,896]{1,0:T(8,128)(2,1)}) %all-gather.8.cloned.1.call-update) | async-done | bytes 6422544 | tf_op jit(solution)/shard_map/all_gather | solution.py:58
  429.7 7.0 %multiply_reduce_fusion.3 = (f32[896]{0:T(1024)S(1)}, f32[896]{0:T(1024)S(1)}, f32[896]{0:T(1024)S(1)}, f32[896]{0:T(1024)S(1)}, f32[112,896]{1,0:T(8,128)}) fusion(f32[112,896]{1,0:T(8,128)S(1)} %get-tuple-element.10, f32[112,896]{1,0:T(8,128)S(1)} %get-tuple-element.14, f32[896]{0:T(1024)S(1)} %get-tuple-element.11, ...), kind=kOutput, calls=%fused_computation.17 | convolution fusion | flops 4317340160 | bytes 9451456 | tf_op jit(solution)/shard_map/dot_general | solution.py:60
  436.7 0.2 broadcast_in_dim.13
  437.0 21.5 %all_to_all.13 = f32[32,1,3584]{2,1,0:T(1,128)S(1)} all-to-all(f32[32,1,3584]{2,1,0:T(1,128)S(1)} %broadcast_in_dim.13), channel_id=1, replica_groups=mesh['row_0'=4,'row_1'=8,'col'=8] {'row_0','row_1'}, dimensions={0} | all-to-all | bytes 917504 | tf_op jit(solution)/shard_map/all_to_all | solution.py:19
  458.5 0.3 reduce_sum.103
  458.8 2.0 multiply_subtract_fusion
  (7 shorter events, 0.1 us)
Async XLA Ops:
  7.2 37.7 %copy-start = (bf16[4,112,896]{2,1,0:T(8,128)(2,1)S(1)}, bf16[4,112,896]{2,1,0:T(8,128)(2,1)}, u32[]{:S(2)}) copy-start(bf16[4,112,896]{2,1,0:T(8,128)(2,1)} %param.3) | copy-start | bytes 2408452
  7.2 37.7 %all-gather.4.cloned.1.call-start = ((), (), s32[]{:S(2)}) async-start(), calls=%async_computation.4 | async-start | bytes 4128768 | tf_op jit(solution)/shard_map/all_gather | solution.py:40
  9.3 163.8 %reduce-scatter.3.cloned.1.call-start = ((), (), s32[]{:S(2)}) async-start(), calls=%async_computation.5 | async-start | bytes 16056320 | tf_op jit(solution)/shard_map/reduce_scatter | solution.py:13
  53.8 168.3 %reduce-scatter.5.cloned.1.call-start = ((), (), s32[]{:S(2)}) async-start(), calls=%async_computation.6 | async-start | bytes 3612672 | tf_op jit(solution)/shard_map/reduce_scatter | solution.py:13
  173.1 140.9 %all-gather.6.cloned.1.call-start = ((), (), s32[]{:S(2)}) async-start(), calls=%async_computation.7 | async-start | bytes 6623232 | tf_op jit(solution)/shard_map/all_gather | solution.py:58
  223.9 90.1 %copy-start.1 = (bf16[112,896]{1,0:T(8,128)(2,1)S(1)}, bf16[112,896]{1,0:T(8,128)(2,1)}, u32[]{:S(2)}) copy-start(bf16[112,896]{1,0:T(8,128)(2,1)} %get-tuple-element.13) | copy-start | bytes 602116
  223.9 205.8 %all-gather.8.cloned.1.call-start = ((), (), s32[]{:S(2)}) async-start(), calls=%async_computation.8 | async-start | bytes 6623232 | tf_op jit(solution)/shard_map/all_gather | solution.py:58
Sparse Core Ops, SparseCore 0:
  9.8 34.9 all-gather.3
  53.9 119.1 reduce-scatter.2
  175.6 46.4 reduce-scatter.4
  225.1 88.8 all-gather.5
  344.9 84.7 all-gather.7
where the time goes:
time: 468 us; the launch traced here: 467 us
  waiting for transfers between devices  366 us (78%)
  blocking collectives  43.1 us (9%)
  matrix products  23.4 us (5%)
  between operations  13.9 us (3%)
  local copies, waits for them, and re-layouts  11.4 us (2%)
  other arithmetic  9.11 us (2%)
    all_gather x2, waiting for transfers between devices, shards(): shard_piece = lax.all_gather(rounded, ROW, axis=0, tiled=True)  170 us
    reduce_scatter x2, waiting for transfers between devices, sum_by_axis(): so_far = lax.psum_scatter(so_far, axis, scatter_dimension=0, tiled=True)  161 us
    all_to_all x2, blocking collectives, sent_to_all(): return lax.all_to_all(copies, axis, split_axis=0, concat_axis=0, tiled=True)  43.1 us
    all_gather x1, waiting for transfers between devices, shards(): gram_slabs = lax.all_gather(grams, 'col', axis=2, tiled=True)  35.5 us
    dot_general x2, matrix products, shards(): jnp.dot(add_columns, shard_piece.astype(jnp.float32), precision=high)  14 us
  transfers between devices with their start and end apart: 5, of which 5 were waited for; matrix products, arithmetic and copies ran while one was open for 3% of the time, Pallas kernels for 0%

commit v1 on v0

--- a/solution.py
+++ b/solution.py
@@ -6,6 +6,11 @@
 
 ITERS = 2
 ROW = ("row_0", "row_1")
+
+
+def all_parts(x, axis, d):
+    blocks = lax.all_gather(x, axis)
+    return jnp.concatenate(blocks, axis=d)
 
 
 def sum_by_axis(so_far, axes):
@@ -37,7 +42,7 @@
     col_count = weights.shape[2]
     first_row = lax.axis_index(ROW) * slab_rows
     high = lax.Precision.HIGHEST
-    gram_slabs = lax.all_gather(grams, "col", axis=2, tiled=True)
+    gram_slabs = all_parts(grams, "col", 2)
     gram_total = jnp.sum(gram_slabs, axis=0, dtype=jnp.float32)
     square_block = lax.dynamic_slice_in_dim(gram_slabs, first_row, slab_rows, gram_slabs.ndim - 1)
     diag_total = jnp.einsum(

time: 468 us -> 480 us (1.026)
  local copies, waits for them, and re-layouts: 11.4 us -> 24.4 us
    reshape x0 -> x1, local copies, waits for them, and re-layouts: none -> 7.27 us  [all_parts(): return jnp.concatenate(blocks, axis=d)]
    all_gather x0 -> x1, local copies, waits for them, and re-layouts: none -> 5.9 us  [all_parts(): blocks = lax.all_gather(x, axis)]
  transfers between devices with their start and end apart: 5 -> 5, of which waited for: 5 -> 5; matrix products, arithmetic and copies ran while one was open for 3% -> 4% of each run, Pallas kernels for 0% -> 0%
where the time goes in v1:
time: 480 us
  waiting for transfers between devices  364 us (76%)
  blocking collectives  43.1 us (9%)
  local copies, waits for them, and re-layouts  24.4 us (5%)
  matrix products  22.7 us (5%)
  between operations  13.9 us (3%)
  other arithmetic  11.7 us (2%)
    all_gather x2, waiting for transfers between devices, shards(): shard_piece = lax.all_gather(rounded, ROW, axis=0, tiled=True)  165 us
    reduce_scatter x2, waiting for transfers between devices, sum_by_axis(): so_far = lax.psum_scatter(so_far, axis, scatter_dimension=0, tiled=True)  161 us
    all_to_all x2, blocking collectives, sent_to_all(): return lax.all_to_all(copies, axis, split_axis=0, concat_axis=0, tiled=True)  43.1 us
    all_gather x1, waiting for transfers between devices, all_parts(): blocks = lax.all_gather(x, axis)  36.9 us
    dot_general x2, matrix products, shards(): jnp.dot(add_columns, shard_piece.astype(jnp.float32), precision=high)  13.3 us
  transfers between devices with their start and end apart: 5, of which 5 were waited for; matrix products, arithmetic and copies ran while one was open for 4% of the time, Pallas kernels for 0%

profile of v1, /device:TPU:32, one launch (start us, length us, event | category | flops | bytes accessed | tf_op | source)
XLA Modules:
  0.0 479.7 jit_solution(3525682709833051854)
XLA Ops:
  7.2 0.0 copy-start
  7.2 0.0 all-gather.9.cloned.1.call-start
  7.2 0.7 all-gather.9.cloned.1.call-update
  7.9 0.0 reduce-scatter.3.cloned.1.call-start
  8.0 36.9 %all-gather.9.cloned.1.call-done = bf16[32,112,448]{2,1,0:T(8,128)(2,1)} async-done(((bf16[4,112,448]{2,1,0:T(8,128)(2,1)}), bf16[32,112,448]{2,1,0:T(8,128)(2,1)}) %all-gather.9.cloned.1.call-update) | async-done | bytes 3211280 | tf_op jit(solution)/shard_map/all_gather | solution.py:12
  44.9 5.9 %copy.36 = bf16[8,4,112,448]{3,0,2,1:T(8,128)(2,1)} copy(bf16[8,4,112,448]{3,2,1,0:T(8,128)(2,1)} %bitcast.26) | data formatting | bytes 6422528 | tf_op jit(solution)/shard_map/all_gather | solution.py:12
  50.8 7.3 %reshape.27 = bf16[4,112,3584]{2,1,0:T(8,128)(2,1)} reshape(bf16[4,112,8,448]{3,2,1,0:T(8,128)(2,1)} %bitcast.28) | data formatting | bytes 6422528 | tf_op jit(solution)/shard_map/reshape | solution.py:13
  58.0 0.0 copy-done
  58.0 8.7 %convolution_bitcast_fusion = f32[3584,896]{1,0:T(8,128)} fusion(bf16[4,112,3584]{2,1,0:T(8,128)(2,1)} %reshape.27, bf16[4,112,896]{2,1,0:T(8,128)(2,1)S(1)} %copy-done), kind=kOutput, calls=%fused_computation.2 | convolution fusion | flops 2877292544 | bytes 16859136 | tf_op jit(solution)/shard_map/mrk,mrc->kc/dot_general | solution.py:54
  66.8 0.0 reduce-scatter.3.cloned.1.call-update
  66.8 0.0 reduce-scatter.5.cloned.1.call-start
  66.8 119.3 %reduce-scatter.3.cloned.1.call-done = f32[896,896]{1,0:T(8,128)} async-done(((f32[3584,896]{1,0:T(8,128)}), f32[896,896]{1,0:T(8,128)}) %reduce-scatter.3.cloned.1.call-update) | async-done | bytes 3211280 | tf_op jit(solution)/shard_map/reduce_scatter | solution.py:18
  186.1 0.0 reduce-scatter.5.cloned.1.call-update
  186.1 0.0 all-gather.5.cloned.1.call-start
  186.2 1.1 constant_dynamic-slice_fusion.1
  187.2 3.0 copy.13
  190.2 2.9 gather_fusion
  193.1 0.6 fusion.2
  193.7 41.4 %reduce-scatter.5.cloned.1.call-done = f32[112,896]{1,0:T(8,128)} async-done(((f32[896,896]{1,0:T(8,128)}), f32[112,896]{1,0:T(8,128)}) %reduce-scatter.5.cloned.1.call-update) | async-done | bytes 401424 | tf_op jit(solution)/shard_map/reduce_scatter | solution.py:18
  235.1 1.8 fusion.10
  236.8 0.0 all-gather.5.cloned.1.call-update
  236.9 0.2 all-gather.7.cloned.1.call-start
  237.1 5.6 %convert_reduce_fusion = f32[112,8,448]{2,1,0:T(8,128)} fusion(bf16[8,4,112,448]{3,2,1,0:T(8,128)(2,1)} %bitcast.27), kind=kLoop, calls=%fused_computation.3 | loop fusion | flops 2809856 | bytes 4816896 | tf_op jit(solution)/shard_map/reduce_sum | solution.py:46
  242.7 0.0 copy-start.1
  242.7 2.1 reduce_sum.97
  244.8 0.1 constant_dynamic-slice_fusion
  244.9 1.7 gather_fusion.1
  246.6 80.5 %all-gather.5.cloned.1.call-done = bf16[3584,896]{1,0:T(8,128)(2,1)} async-done(((bf16[112,896]{1,0:T(8,128)(2,1)}), bf16[3584,896]{1,0:T(8,128)(2,1)}) %all-gather.5.cloned.1.call-update) | async-done | bytes 6422544 | tf_op jit(solution)/shard_map/all_gather | solution.py:63
  327.1 0.0 copy-done.1
  327.1 6.6 %multiply_reduce_fusion.6 = (f32[896]{0:T(1024)S(1)}, f32[896]{0:T(1024)S(1)}, f32[896]{0:T(1024)S(1)}, f32[112,896]{1,0:T(8,128)}) fusion(f32[112,896]{1,0:T(8,128)S(1)} %get-tuple-element.14, bf16[112,896]{1,0:T(8,128)(2,1)S(1)} %copy-done.1, f32[112]{0:T(128)S(1)} %broadcast_multiply_fusion, f32[112,3584]{1,0:T(8,128)S(1)} %reduce_sum.97, ...), kind=kOutput, calls=%fused_computation.23 | convolution fusion | flops 4316939776 | bytes 9042880 | tf_op jit(solution)/shard_map/dot_general | solution.py:65
  333.7 0.2 broadcast_in_dim.12
  333.9 21.5 %all_to_all.12 = f32[32,1,3584]{2,1,0:T(1,128)S(1)} all-to-all(f32[32,1,3584]{2,1,0:T(1,128)S(1)} %broadcast_in_dim.12), channel_id=1, replica_groups=mesh['row_0'=4,'row_1'=8,'col'=8] {'row_0','row_1'}, dimensions={0} | all-to-all | bytes 917504 | tf_op jit(solution)/shard_map/all_to_all | solution.py:24
  355.5 0.3 reduce_sum.101
  355.8 1.7 fusion.5
  357.5 0.0 all-gather.7.cloned.1.call-update
  357.5 84.9 %all-gather.7.cloned.1.call-done = bf16[3584,896]{1,0:T(8,128)(2,1)} async-done(((bf16[112,896]{1,0:T(8,128)(2,1)}), bf16[3584,896]{1,0:T(8,128)(2,1)}) %all-gather.7.cloned.1.call-update) | async-done | bytes 6422544 | tf_op jit(solution)/shard_map/all_gather | solution.py:63
  442.4 6.7 %multiply_reduce_fusion.3 = (f32[896]{0:T(1024)S(1)}, f32[896]{0:T(1024)S(1)}, f32[896]{0:T(1024)S(1)}, f32[896]{0:T(1024)S(1)}, f32[112,896]{1,0:T(8,128)}) fusion(f32[112,896]{1,0:T(8,128)S(1)} %get-tuple-element.10, f32[112,896]{1,0:T(8,128)S(1)} %get-tuple-element.14, f32[896]{0:T(1024)S(1)} %get-tuple-element.11, ...), kind=kOutput, calls=%fused_computation.18 | convolution fusion | flops 4317340160 | bytes 9451456 | tf_op jit(solution)/shard_map/dot_general | solution.py:65
  449.1 0.2 broadcast_in_dim.13
  449.4 21.5 %all_to_all.13 = f32[32,1,3584]{2,1,0:T(1,128)S(1)} all-to-all(f32[32,1,3584]{2,1,0:T(1,128)S(1)} %broadcast_in_dim.13), channel_id=1, replica_groups=mesh['row_0'=4,'row_1'=8,'col'=8] {'row_0','row_1'}, dimensions={0} | all-to-all | bytes 917504 | tf_op jit(solution)/shard_map/all_to_all | solution.py:24
  470.9 0.3 reduce_sum.106
  471.2 2.0 multiply_subtract_fusion
  (6 shorter events, 0.0 us)
Async XLA Ops:
  7.2 50.9 %copy-start = (bf16[4,112,896]{2,1,0:T(8,128)(2,1)S(1)}, bf16[4,112,896]{2,1,0:T(8,128)(2,1)}, u32[]{:S(2)}) copy-start(bf16[4,112,896]{2,1,0:T(8,128)(2,1)} %param.3) | copy-start | bytes 2408452
  7.2 37.7 %all-gather.9.cloned.1.call-start = ((), (), s32[]{:S(2)}) async-start(), calls=%async_computation.8 | async-start | bytes 4128768 | tf_op jit(solution)/shard_map/all_gather | solution.py:12
  7.9 178.2 %reduce-scatter.3.cloned.1.call-start = ((), (), s32[]{:S(2)}) async-start(), calls=%async_computation.4 | async-start | bytes 16056320 | tf_op jit(solution)/shard_map/reduce_scatter | solution.py:18
  66.8 168.3 %reduce-scatter.5.cloned.1.call-start = ((), (), s32[]{:S(2)}) async-start(), calls=%async_computation.5 | async-start | bytes 3612672 | tf_op jit(solution)/shard_map/reduce_scatter | solution.py:18
  186.1 140.9 %all-gather.5.cloned.1.call-start = ((), (), s32[]{:S(2)}) async-start(), calls=%async_computation.6 | async-start | bytes 6623232 | tf_op jit(solution)/shard_map/all_gather | solution.py:63
  236.9 205.6 %all-gather.7.cloned.1.call-start = ((), (), s32[]{:S(2)}) async-start(), calls=%async_computation.7 | async-start | bytes 6623232 | tf_op jit(solution)/shard_map/all_gather | solution.py:63
  242.7 84.3 %copy-start.1 = (bf16[112,896]{1,0:T(8,128)(2,1)S(1)}, bf16[112,896]{1,0:T(8,128)(2,1)}, u32[]{:S(2)}) copy-start(bf16[112,896]{1,0:T(8,128)(2,1)} %get-tuple-element.13) | copy-start | bytes 602116
Sparse Core Ops, SparseCore 0:
  9.8 34.9 all-gather.8
  66.9 119.1 reduce-scatter.2
  188.7 46.3 reduce-scatter.4
  238.1 88.9 all-gather.4
  357.7 84.7 all-gather.6
